TPU v7x, 32 devices: a whole 2x2x4 slice. The times are simulated.
32 devices in a mesh: dp: 16 (over z, y, core), local: 2 (over x).
Axes of the slice: x: 2, y: 2, z: 4, core: 2. Of those that a mesh axis runs over, the one named last changes fastest.
Arguments:
- pre_glu: bfloat16 [32, 256, 3072], P(('dp', 'local')), may hold values from -80 to 80
- lengths: int32 [32], P(('dp', 'local')), may hold values from 1 to 256, as said below
- kernel: float32 [5, 1536], replicated, may hold values from -2.5 to 2.5
- bn_gain: float32 [1536], replicated, may hold values from 0.5 to 2
- bn_shift: float32 [1536], replicated, may hold values from -1 to 1
- w_out: bfloat16 [1536, 1536], replicated, may hold values from -0.15625 to 0.15625
- cotangent: bfloat16 [32, 256, 1536], P(('dp', 'local')), may hold values from -6 to 6
Outputs:
- grad_pre_glu: bfloat16 [32, 256, 3072], P(('dp', 'local'))
- grad_w_out: float32 [1536, 1536], P('dp', 'local')
- grad_kernel: float32 [5, 1536], replicated
- grad_gain: float32 [1536], replicated
- grad_shift: float32 [1536], replicated
Inputs may be any that keep to these rules, and one draw needn't show every extreme that they name: `lengths`: each utterance's valid frames are its first ones; some utterance has all 256 frames valid.
All inputs are finite; a program needn't handle non-finite values.
Results may differ from a plain program's by a relative error of at most 0.0029.
Values sent between devices are 32-bit elements; how exact they have to be, the bound alone decides.
A program may use at most 64 MiB of HBM per device.

v0:
```python
import jax
import jax.numpy as jnp
from jax import lax
from jax.sharding import PartitionSpec as P

epsilon = 1e-05


def on_device(pre_glu, lengths, kernel, bn_gain, bn_shift, w_out, cotangent):
    frames = pre_glu.shape[1]
    model_width = kernel.shape[1]
    kernel_taps = kernel.shape[0]
    half_width = (kernel_taps - 1) // 2
    replicas = lax.axis_size("dp") * lax.axis_size("local")
    valid_mask = (jnp.arange(frames, dtype=jnp.int32)[:, None] < lengths[0]).astype(jnp.float32)
    first_half = pre_glu[0, :, :model_width].astype(jnp.float32)
    gate_value = jax.nn.sigmoid(pre_glu[0, :, model_width:].astype(jnp.float32))
    glu_out = first_half * gate_value * valid_mask
    padded = jnp.pad(glu_out, ((half_width, half_width), (0, 0)))
    conv_out = kernel[0] * padded[0:frames]
    for j in range(1, kernel_taps):
        conv_out = conv_out + kernel[j] * padded[j : j + frames]
    own_count = lengths[0].astype(jnp.float32)
    sum_first, sum_square, frame_total = lax.psum(
        (
            jnp.sum(conv_out * valid_mask, 0),
            jnp.sum(conv_out * conv_out * valid_mask, 0),
            own_count,
        ),
        ("dp", "local"),
    )
    mean_value = sum_first / frame_total
    variance = sum_square / frame_total - mean_value * mean_value
    invstd = lax.rsqrt(variance + epsilon)
    normed = (conv_out - mean_value) * invstd
    act_in = bn_gain * normed + bn_shift
    sig_act = jax.nn.sigmoid(act_in)
    swished = (act_in * sig_act).astype(jnp.bfloat16)
    masked_cot = cotangent[0] * valid_mask.astype(jnp.bfloat16)
    contract = (((0,), (0,)), ((), ()))
    wgrad_term = lax.dot_general(swished, masked_cot, contract, preferred_element_type=jnp.float32)
    partial_value = lax.psum_scatter(wgrad_term, "dp", scatter_dimension=0, tiled=True)
    weight_shard = lax.psum_scatter(partial_value, "local", scatter_dimension=1, tiled=True)
    grad_swish = lax.dot_general(
        masked_cot, w_out, (((1,), (1,)), ((), ())), preferred_element_type=jnp.float32
    )
    grad_act = grad_swish * sig_act * (1.0 + act_in * (1.0 - sig_act))
    channel_scale = bn_gain * invstd
    sum_shift, sum_gain = lax.psum(
        (jnp.sum(grad_act, 0), jnp.sum(grad_act * normed, 0)), ("dp", "local")
    )
    grad_conv = (
        valid_mask * channel_scale * (grad_act - (sum_shift + normed * sum_gain) / frame_total)
    )
    kernel_part = jnp.stack(
        [jnp.sum(grad_conv * padded[j : j + frames], 0) for j in range(kernel_taps)], 0
    )
    kernel_sum = lax.psum(kernel_part, ("dp", "local"))
    grad_padded = jnp.pad(grad_conv, ((half_width, half_width), (0, 0)))
    grad_glu = kernel[0] * grad_padded[kernel_taps - 1 : kernel_taps - 1 + frames]
    for j in range(1, kernel_taps):
        grad_glu = (
            grad_glu + kernel[j] * grad_padded[kernel_taps - 1 - j : kernel_taps - 1 - j + frames]
        )
    grad_glu = grad_glu * valid_mask
    grad_first = grad_glu * gate_value
    grad_second = grad_glu * first_half * gate_value * (1.0 - gate_value)
    grad_pre = jnp.concatenate([grad_first, grad_second], 1).astype(jnp.bfloat16)[None]
    return (
        grad_pre,
        weight_shard / replicas,
        kernel_sum / replicas,
        sum_gain / replicas,
        sum_shift / replicas,
    )


def solution(mesh):
    return jax.shard_map(
        on_device,
        mesh=mesh,
        in_specs=(
            P(("dp", "local"), None, None),
            P(("dp", "local")),
            P(),
            P(),
            P(),
            P(),
            P(("dp", "local"), None, None),
        ),
        out_specs=(P(("dp", "local"), None, None), P("dp", "local"), P(), P(), P()),
        check_vma=False,
    )
```

profile of v0, /device:TPU:0, one launch (start us, length us, event | category | flops | bytes accessed | tf_op | source)
XLA Modules:
  0.0 228.4 jit_solution(6184416316779539486)
XLA Ops:
  7.2 0.0 reduce-scatter.3.cloned.1.call-start
  7.9 1.1 slice_reduce_fusion.4
  9.0 1.8 fusion.1
  10.8 0.0 copy-start.2
  10.8 0.0 copy-start.3
  10.8 1.1 multiply_reduce_fusion.7
  11.9 42.4 %all-reduce.3 = (f32[1536]{0:T(1024)S(1)}, f32[]{:T(128)}, f32[1536]{0:T(1024)S(1)}) all-reduce(f32[1536]{0:T(1024)S(1)} %get-tuple-element.11, f32[]{:T(128)S(6)} %convert_element_type.50, f32[1536]{0:T(1024)S(1)} %get-tuple-element.10), channel_id=1, replica_groups=mesh['dp'=16,'local'=2] {'dp','local'}, use_global_device_ids=true, to_apply=%region_4.5 | all-reduce | flops 3073 | bytes 24584 | tf_op jit(solution)/shard_map/psum | solution.py:24
  54.4 0.0 copy-done.2
  54.4 0.7 fusion.17
  55.0 0.7 add_rsqrt_fusion
  55.7 0.0 copy-done.3
  55.7 6.4 %fusion.7 = f32[1536,1536]{1,0:T(8,128)} fusion(f32[256,1536]{1,0:T(8,128)S(1)} %get-tuple-element.29, f32[1536]{0:T(1024)S(1)} %copy-done.3, f32[1536]{0:T(1024)S(1)} %add_rsqrt_fusion, f32[1536]{0:T(1024)S(1)} %get-tuple-element.28, f32[1536]{0:T(1024)S(1)} %copy-done.2, bf16[1,256,1536]{2,1,0:T(8,128)(2,1)} %param.13, bf16[256]{0:T(256)(128)(2,1)S(1)} %fusion.18), kind=kOutput, calls=%fused_computation.33 | convolution fusion | flops 1211891712 | bytes 11821568 | tf_op jit(solution)/shard_map/dot_general | solution.py:41
  62.1 0.0 reduce-scatter.3.cloned.1.call-update
  62.2 0.0 reduce-scatter.5.cloned.1.call-start
  62.2 5.6 %fusion.20 = (f32[1536]{0:T(1024)S(1)}, f32[1536]{0:T(1024)S(1)}, f32[256,1536]{1,0:T(8,128)}) fusion(f32[1536]{0:T(1024)S(1)} %add_rsqrt_fusion, f32[256,1536]{1,0:T(8,128)S(1)} %get-tuple-element.29, f32[1536]{0:T(1024)S(1)} %get-tuple-element.28, f32[1536]{0:T(1024)S(1)} %copy-done.3, f32[1536]{0:T(1024)S(1)} %copy-done.2, ...), kind=kOutput, calls=%fused_computation.60 | convolution fusion | flops 1214247936 | bytes 8688128 | tf_op jit(solution)/shard_map/dot_general | solution.py:44
  67.8 41.1 %all-reduce.2 = (f32[1536]{0:T(1024)S(1)}, f32[1536]{0:T(1024)S(1)}) all-reduce(f32[1536]{0:T(1024)S(1)} %get-tuple-element.13, f32[1536]{0:T(1024)S(1)} %get-tuple-element.12), channel_id=1, replica_groups=mesh['dp'=16,'local'=2] {'dp','local'}, use_global_device_ids=true, to_apply=%region_8.9 | all-reduce | flops 3072 | bytes 24576 | tf_op jit(solution)/shard_map/psum | solution.py:49
  108.9 0.0 copy-start
  108.9 3.5 %multiply_reduce_fusion = (f32[1536]{0:T(1024)S(1)}, f32[1536]{0:T(1024)S(1)}, f32[1536]{0:T(1024)S(1)}, f32[1536]{0:T(1024)S(1)}, f32[1536]{0:T(1024)S(1)}, /*index=5*/f32[256,1536]{1,0:T(8,128)S(1)}) fusion(f32[256,1536]{1,0:T(8,128)S(1)} %fusion.1, f32[256,1536]{1,0:T(8,128)} %get-tuple-element.30, f32[]{:T(128)} %get-tuple-element.22, ...), kind=kLoop, calls=%fused_computation.12 | loop fusion | flops 7070208 | bytes 6353924 | tf_op jit(solution)/shard_map/reduce_sum | solution.py:56
  112.4 0.0 copy-done
  112.4 0.0 copy-start.1
  112.4 2.2 fusion.8
  114.6 59.1 %reduce-scatter.3.cloned.1.call-done = f32[96,1536]{1,0:T(8,128)} async-done(((f32[1536,1536]{1,0:T(8,128)}), f32[96,1536]{1,0:T(8,128)}) %reduce-scatter.3.cloned.1.call-update) | async-done | bytes 589840 | tf_op jit(solution)/shard_map/reduce_scatter | solution.py:42
  173.7 0.0 reduce-scatter.5.cloned.1.call-update
  173.7 0.0 copy-done.1
  173.7 1.4 fusion.9
  175.2 0.1 stack.23
  175.2 40.7 %psum.47 = f32[5,1536]{1,0:T(8,128)S(1)} all-reduce(f32[5,1536]{1,0:T(8,128)S(1)} %stack.23), channel_id=1, replica_groups=mesh['dp'=16,'local'=2] {'dp','local'}, use_global_device_ids=true, to_apply=%region_16.17 | all-reduce | flops 7680 | bytes 61440 | tf_op jit(solution)/shard_map/psum | solution.py:58
  216.0 0.6 broadcast_multiply_fusion.2
  216.6 2.7 %pad_maximum_fusion = bf16[1,256,3072]{2,1,0:T(8,128)(2,1)} fusion(bf16[1,256,1536]{2,1,0:T(8,128)(2,1)} %fusion.9, bf16[1,256,1536]{2,1,0:T(8,128)(2,1)} %get-tuple-element.25), kind=kLoop, calls=%fused_computation.8 | loop fusion | flops 3145728 | bytes 3145728 | tf_op jit(solution)/shard_map/concatenate | solution.py:68
  219.2 0.6 broadcast_multiply_fusion.1
  219.9 0.0 reduce-scatter.5.cloned.1.call-done
  219.9 1.7 broadcast_multiply_fusion
  (7 shorter events, 0.0 us)
Async XLA Ops:
  7.2 166.5 %reduce-scatter.3.cloned.1.call-start = ((), (), s32[]{:S(2)}) async-start(), calls=%async_computation.2 | async-start | bytes 10027008 | tf_op jit(solution)/shard_map/reduce_scatter | solution.py:42
  10.8 43.6 %copy-start.2 = (f32[1536]{0:T(1024)S(1)}, f32[1536]{0:T(1024)}, u32[]{:S(2)}) copy-start(f32[1536]{0:T(1024)} %param.10) | copy-start | bytes 18436
  10.8 44.9 %copy-start.3 = (f32[1536]{0:T(1024)S(1)}, f32[1536]{0:T(1024)}, u32[]{:S(2)}) copy-start(f32[1536]{0:T(1024)} %param.11) | copy-start | bytes 18436
  62.2 157.7 %reduce-scatter.5.cloned.1.call-start = ((), (), s32[]{:S(2)}) async-start(), calls=%async_computation.3 | async-start | bytes 884736 | tf_op jit(solution)/shard_map/reduce_scatter | solution.py:43
  108.9 3.5 %copy-start = (bf16[1,256,3072]{2,1,0:T(8,128)(2,1)S(1)}, bf16[1,256,3072]{2,1,0:T(8,128)(2,1)}, u32[]{:S(2)}) copy-start(bf16[1,256,3072]{2,1,0:T(8,128)(2,1)} %param.7) | copy-start | bytes 4718596
  112.4 61.3 %copy-start.1 = (bf16[1,256,3072]{2,1,0:T(8,128)(2,1)S(1)}, bf16[1,256,3072]{2,1,0:T(8,128)(2,1)}, u32[]{:S(2)}) copy-start(bf16[1,256,3072]{2,1,0:T(8,128)(2,1)} %param.7) | copy-start | bytes 4718596
Sparse Core Ops, SparseCore 0:
  62.3 111.3 reduce-scatter.2
  175.9 15.2 reduce-scatter.4
where the time goes:
time: 229 us; the launch traced here: 228 us
  blocking collectives  124 us (54%)
  waiting for transfers between devices  59.1 us (26%)
  other arithmetic  16.9 us (7%)
  between operations  14.8 us (6%)
  matrix products  12 us (5%)
    reduce_scatter x1, waiting for transfers between devices, on_device(): lax.psum_scatter(wgrad_term, 'dp', scatter_dimension=0, tiled=True)  59.1 us
    psum x1, blocking collectives, on_device(): lax.psum((jnp.sum(conv_out * valid_mask, 0), jnp.sum(conv_out * conv_out...  42.4 us
    psum x1, blocking collectives, on_device(): lax.psum((jnp.sum(grad_act, 0), jnp.sum(grad_act * normed, 0)), ('dp', 'l...  41.1 us
    psum x1, blocking collectives, on_device(): kernel_sum = lax.psum(kernel_part, ('dp', 'local'))  40.7 us
    dot_general x1, matrix products, on_device(): lax.dot_general(swished, masked_cot, contract, preferred_element_type=jnp...  6.43 us
    concatenate x3, other arithmetic, on_device(): jnp.concatenate([grad_first, grad_second], 1).astype(jnp.bfloat16)[None]  6.24 us
    dot_general x1, matrix products, on_device(): lax.dot_general(masked_cot, w_out, (((1,), (1,)), ((), ())), preferred_el...  5.56 us
  transfers between devices with their start and end apart: 2, of which 1 were waited for; matrix products, arithmetic and copies ran while one was open for 7% of the time, Pallas kernels for 0%

commit v1 on v0

--- a/solution.py
+++ b/solution.py
@@ -55,7 +55,7 @@
     kernel_part = jnp.stack(
         [jnp.sum(grad_conv * padded[j : j + frames], 0) for j in range(kernel_taps)], 0
     )
-    kernel_sum = lax.psum(kernel_part, ("dp", "local"))
+    kernel_sum = lax.psum(lax.psum(kernel_part, "local"), "dp")
     grad_padded = jnp.pad(grad_conv, ((half_width, half_width), (0, 0)))
     grad_glu = kernel[0] * grad_padded[kernel_taps - 1 : kernel_taps - 1 + frames]
     for j in range(1, kernel_taps):

time: 229 us -> 255 us (1.11)
  blocking collectives: 124 us -> 150 us
    psum x1 -> x2, blocking collectives: 40.7 us -> 66.8 us  [on_device(): kernel_sum = lax.psum(lax.psum(kernel_part, 'local'), 'dp')]
where the time goes in v1:
time: 255 us
  blocking collectives  150 us (59%)
  waiting for transfers between devices  59.1 us (23%)
  other arithmetic  16.9 us (7%)
  between operations  14.8 us (6%)
  matrix products  12 us (5%)
    psum x2, blocking collectives, on_device(): kernel_sum = lax.psum(lax.psum(kernel_part, 'local'), 'dp')  66.8 us
    reduce_scatter x1, waiting for transfers between devices, on_device(): lax.psum_scatter(wgrad_term, 'dp', scatter_dimension=0, tiled=True)  59.1 us
    psum x1, blocking collectives, on_device(): lax.psum((jnp.sum(conv_out * valid_mask, 0), jnp.sum(conv_out * conv_out...  42.4 us
    psum x1, blocking collectives, on_device(): lax.psum((jnp.sum(grad_act, 0), jnp.sum(grad_act * normed, 0)), ('dp', 'l...  41.1 us
    dot_general x1, matrix products, on_device(): lax.dot_general(swished, masked_cot, contract, preferred_element_type=jnp...  6.43 us
    concatenate x3, other arithmetic, on_device(): jnp.concatenate([grad_first, grad_second], 1).astype(jnp.bfloat16)[None]  6.24 us
    dot_general x1, matrix products, on_device(): lax.dot_general(masked_cot, w_out, (((1,), (1,)), ((), ())), preferred_el...  5.56 us
  transfers between devices with their start and end apart: 2, of which 1 were waited for; matrix products, arithmetic and copies ran while one was open for 7% of the time, Pallas kernels for 0%

profile of v1, /device:TPU:0, one launch (start us, length us, event | category | flops | bytes accessed | tf_op | source)
XLA Modules:
  0.0 254.5 jit_solution(5717683161923721577)
XLA Ops:
  7.2 0.0 reduce-scatter.3.cloned.1.call-start
  7.9 1.1 slice_reduce_fusion.4
  9.0 1.8 fusion.1
  10.8 0.0 copy-start.2
  10.8 0.0 copy-start.3
  10.8 1.1 multiply_reduce_fusion.7
  11.9 42.4 %all-reduce.3 = (f32[1536]{0:T(1024)S(1)}, f32[]{:T(128)}, f32[1536]{0:T(1024)S(1)}) all-reduce(f32[1536]{0:T(1024)S(1)} %get-tuple-element.11, f32[]{:T(128)S(6)} %convert_element_type.50, f32[1536]{0:T(1024)S(1)} %get-tuple-element.10), channel_id=1, replica_groups=mesh['dp'=16,'local'=2] {'dp','local'}, use_global_device_ids=true, to_apply=%region_4.5 | all-reduce | flops 3073 | bytes 24584 | tf_op jit(solution)/shard_map/psum | solution.py:24
  54.4 0.0 copy-done.2
  54.4 0.7 fusion.17
  55.0 0.7 add_rsqrt_fusion
  55.7 0.0 copy-done.3
  55.7 6.4 %fusion.7 = f32[1536,1536]{1,0:T(8,128)} fusion(f32[256,1536]{1,0:T(8,128)S(1)} %get-tuple-element.29, f32[1536]{0:T(1024)S(1)} %copy-done.3, f32[1536]{0:T(1024)S(1)} %add_rsqrt_fusion, f32[1536]{0:T(1024)S(1)} %get-tuple-element.28, f32[1536]{0:T(1024)S(1)} %copy-done.2, bf16[1,256,1536]{2,1,0:T(8,128)(2,1)} %param.13, bf16[256]{0:T(256)(128)(2,1)S(1)} %fusion.18), kind=kOutput, calls=%fused_computation.33 | convolution fusion | flops 1211891712 | bytes 11821568 | tf_op jit(solution)/shard_map/dot_general | solution.py:41
  62.1 0.0 reduce-scatter.3.cloned.1.call-update
  62.2 0.0 reduce-scatter.5.cloned.1.call-start
  62.2 5.6 %fusion.20 = (f32[1536]{0:T(1024)S(1)}, f32[1536]{0:T(1024)S(1)}, f32[256,1536]{1,0:T(8,128)}) fusion(f32[1536]{0:T(1024)S(1)} %add_rsqrt_fusion, f32[256,1536]{1,0:T(8,128)S(1)} %get-tuple-element.29, f32[1536]{0:T(1024)S(1)} %get-tuple-element.28, f32[1536]{0:T(1024)S(1)} %copy-done.3, f32[1536]{0:T(1024)S(1)} %copy-done.2, ...), kind=kOutput, calls=%fused_computation.60 | convolution fusion | flops 1214247936 | bytes 8688128 | tf_op jit(solution)/shard_map/dot_general | solution.py:44
  67.8 41.1 %all-reduce.2 = (f32[1536]{0:T(1024)S(1)}, f32[1536]{0:T(1024)S(1)}) all-reduce(f32[1536]{0:T(1024)S(1)} %get-tuple-element.13, f32[1536]{0:T(1024)S(1)} %get-tuple-element.12), channel_id=1, replica_groups=mesh['dp'=16,'local'=2] {'dp','local'}, use_global_device_ids=true, to_apply=%region_8.9 | all-reduce | flops 3072 | bytes 24576 | tf_op jit(solution)/shard_map/psum | solution.py:49
  108.9 0.0 copy-start
  108.9 3.5 %multiply_reduce_fusion = (f32[1536]{0:T(1024)S(1)}, f32[1536]{0:T(1024)S(1)}, f32[1536]{0:T(1024)S(1)}, f32[1536]{0:T(1024)S(1)}, f32[1536]{0:T(1024)S(1)}, /*index=5*/f32[256,1536]{1,0:T(8,128)S(1)}) fusion(f32[256,1536]{1,0:T(8,128)S(1)} %fusion.1, f32[256,1536]{1,0:T(8,128)} %get-tuple-element.30, f32[]{:T(128)} %get-tuple-element.22, ...), kind=kLoop, calls=%fused_computation.12 | loop fusion | flops 7070208 | bytes 6353924 | tf_op jit(solution)/shard_map/reduce_sum | solution.py:56
  112.4 0.0 copy-done
  112.4 0.0 copy-start.1
  112.4 2.2 fusion.8
  114.6 59.1 %reduce-scatter.3.cloned.1.call-done = f32[96,1536]{1,0:T(8,128)} async-done(((f32[1536,1536]{1,0:T(8,128)}), f32[96,1536]{1,0:T(8,128)}) %reduce-scatter.3.cloned.1.call-update) | async-done | bytes 589840 | tf_op jit(solution)/shard_map/reduce_scatter | solution.py:42
  173.7 0.0 reduce-scatter.5.cloned.1.call-update
  173.7 0.0 copy-done.1
  173.7 1.4 fusion.9
  175.2 0.1 stack.23
  175.2 9.1 %psum.54 = f32[5,1536]{1,0:T(8,128)S(1)} all-reduce(f32[5,1536]{1,0:T(8,128)S(1)} %stack.23), channel_id=1, replica_groups=mesh['dp'=16,'local'=2] {'local'}, use_global_device_ids=true, to_apply=%region_16.17 | all-reduce | flops 7680 | bytes 61440 | tf_op jit(solution)/shard_map/psum | solution.py:58
  184.4 57.7 %psum.55 = f32[5,1536]{1,0:T(8,128)S(1)} all-reduce(f32[5,1536]{1,0:T(8,128)S(1)} %psum.54), channel_id=1, replica_groups=mesh['dp'=16,'local'=2] {'dp'}, use_global_device_ids=true, to_apply=%region_17.18 | all-reduce | flops 7680 | bytes 61440 | tf_op jit(solution)/shard_map/psum | solution.py:58
  242.1 0.6 broadcast_multiply_fusion.2
  242.7 2.7 %pad_maximum_fusion = bf16[1,256,3072]{2,1,0:T(8,128)(2,1)} fusion(bf16[1,256,1536]{2,1,0:T(8,128)(2,1)} %fusion.9, bf16[1,256,1536]{2,1,0:T(8,128)(2,1)} %get-tuple-element.25), kind=kLoop, calls=%fused_computation.8 | loop fusion | flops 3145728 | bytes 3145728 | tf_op jit(solution)/shard_map/concatenate | solution.py:68
  245.3 0.6 broadcast_multiply_fusion.1
  246.0 1.7 broadcast_multiply_fusion
  (8 shorter events, 0.0 us)
Async XLA Ops:
  7.2 166.5 %reduce-scatter.3.cloned.1.call-start = ((), (), s32[]{:S(2)}) async-start(), calls=%async_computation.2 | async-start | bytes 10027008 | tf_op jit(solution)/shard_map/reduce_scatter | solution.py:42
  10.8 43.6 %copy-start.2 = (f32[1536]{0:T(1024)S(1)}, f32[1536]{0:T(1024)}, u32[]{:S(2)}) copy-start(f32[1536]{0:T(1024)} %param.10) | copy-start | bytes 18436
  10.8 44.9 %copy-start.3 = (f32[1536]{0:T(1024)S(1)}, f32[1536]{0:T(1024)}, u32[]{:S(2)}) copy-start(f32[1536]{0:T(1024)} %param.11) | copy-start | bytes 18436
  62.2 183.8 %reduce-scatter.5.cloned.1.call-start = ((), (), s32[]{:S(2)}) async-start(), calls=%async_computation.3 | async-start | bytes 884736 | tf_op jit(solution)/shard_map/reduce_scatter | solution.py:43
  108.9 3.5 %copy-start = (bf16[1,256,3072]{2,1,0:T(8,128)(2,1)S(1)}, bf16[1,256,3072]{2,1,0:T(8,128)(2,1)}, u32[]{:S(2)}) copy-start(bf16[1,256,3072]{2,1,0:T(8,128)(2,1)} %param.7) | copy-start | bytes 4718596
  112.4 61.3 %copy-start.1 = (bf16[1,256,3072]{2,1,0:T(8,128)(2,1)S(1)}, bf16[1,256,3072]{2,1,0:T(8,128)(2,1)}, u32[]{:S(2)}) copy-start(bf16[1,256,3072]{2,1,0:T(8,128)(2,1)} %param.7) | copy-start | bytes 4718596
Sparse Core Ops, SparseCore 0:
  62.3 111.3 reduce-scatter.2
  175.9 15.2 reduce-scatter.4
